TPU v7x, 512 devices: a 4x2x32 block of a 4x8x32 slice. The times are simulated.
512 devices in a mesh: group: 2 (over y), seq: 32 (over z), head: 4 (over x), sub: 2 (over core).
Axes of the slice: x: 4, y: 2, z: 32, core: 2. Of those that a mesh axis runs over, the one named last changes fastest.
The devices are a block of a 4x8x32 slice.
Arguments:
- queries: bfloat16 [32, 32, 128], P(('group', 'sub'), 'head'), parts along dimension 0, may hold values from -8 to 8
- lengths: int32 [32], P(('group', 'sub')), parts along dimension 0, may hold values from 1 to 192, 2048 in all
- k_cache: bfloat16 [524288, 8, 128], P(('group', 'seq', 'sub'), 'head'), parts along dimension 0, may hold values from -12 to 12
- v_cache: bfloat16 [524288, 8, 128], P(('group', 'seq', 'sub'), 'head'), parts along dimension 0, may hold values from -6 to 6
Outputs:
- attended: bfloat16 [32, 32, 128], P('group', ('head', 'sub')), parts along dimension 0
There are 2 independent parts, one for each index of `group`. A program takes and returns all parts, laid end to end along the dimension named above; each array names one. Nothing has to cross between parts.
Inputs may be any that keep to these rules, and one draw needn't show every extreme that they name: The lengths sum to exactly 2048, and some request has exactly 192 pages.
All inputs are finite; a program needn't handle non-finite values. No bound on the sum of `lengths` on one device may be relied on, other than what follows from the above.
Results may differ from a plain program's by a relative error of at most 0.0044.
Values may be sent and summed in bfloat16 or wider, within the bound.
A program may use at most 64 MiB of HBM per device.

v0:
```python
import functools

import jax
import jax.numpy as jnp
from jax import lax
from jax.sharding import PartitionSpec as P

PAGE = 128


lowest_score = -1e30


def laid_out(pieces, dim):
    pieces = jnp.moveaxis(pieces, 0, dim)
    shape = pieces.shape
    return pieces.reshape(*shape[:dim], shape[dim] * shape[dim + 1], *shape[dim + 2 :])


def sent_to_all(x, axis):
    copies = jnp.broadcast_to(x, (lax.axis_size(axis), *x.shape))
    return lax.all_to_all(copies, axis, split_axis=0, concat_axis=0, tiled=True)


def gathered_copies(x, axis, dim):
    return laid_out(sent_to_all(x, axis), dim)


def one_axis_at_a_time(x, axes):
    return functools.reduce(lax.pmax, axes, x)


def gathered_total(x, axis):
    pieces = lax.all_gather(x, axis)
    return pieces.sum(axis=0)


def shards(queries, lengths, k_cache, v_cache):
    tokens_local = k_cache.shape[0]
    key_heads = k_cache.shape[1]
    head_width = k_cache.shape[2]
    query_heads = queries.shape[1]
    group_size = query_heads // key_heads
    pages_local = tokens_local // PAGE
    every_query = gathered_copies(queries, "sub", 0)
    request_count = every_query.shape[0]
    counts = gathered_copies(lengths, "sub", 0)
    starts = jnp.cumsum(counts) - counts
    position = lax.axis_index(("seq", "sub"))
    page_ids = position * pages_local + jnp.arange(pages_local, dtype=jnp.int32)
    owner = jnp.sum((starts[None, :] <= page_ids[:, None]).astype(jnp.int32), axis=1) - 1
    page_query = jnp.take(every_query, owner, axis=0).reshape(
        pages_local, key_heads, group_size, head_width
    )
    key_pages = k_cache.reshape(pages_local, PAGE, key_heads, head_width)
    value_pages = v_cache.reshape(pages_local, PAGE, key_heads, head_width)
    scores = jnp.einsum(
        "pskd,pkgd->pkgs", key_pages, page_query, preferred_element_type=jnp.float32
    ) * float(head_width) ** (-0.5)
    page_max = jnp.max(scores, axis=3)
    weights = jnp.exp(scores - page_max[..., None])
    page_sum = jnp.sum(weights, axis=3)
    page_out = jnp.einsum(
        "pkgs,pskd->pkgd",
        weights.astype(jnp.bfloat16),
        value_pages,
        preferred_element_type=jnp.float32,
    )
    member = owner[:, None] == jnp.arange(request_count, dtype=jnp.int32)[None, :]
    local_max = jnp.max(
        jnp.where(member[:, :, None, None], page_max[:, None], lowest_score), axis=0
    )
    rescale = jnp.exp(page_max - jnp.take(local_max, owner, axis=0))
    member_float = member.astype(jnp.float32)
    dense_sum = jnp.einsum(
        "pr,pkg->rkg", member_float, rescale * page_sum, precision=lax.Precision.HIGHEST
    ).reshape(request_count, query_heads)
    dense_out = jnp.einsum(
        "pr,pkgd->rkgd",
        member_float,
        rescale[..., None] * page_out,
        precision=lax.Precision.HIGHEST,
    ).reshape(request_count, query_heads, head_width)
    dense_max = local_max.reshape(request_count, query_heads)
    own_heads = query_heads // lax.axis_size("sub")
    head_start = lax.axis_index("sub") * own_heads
    top = one_axis_at_a_time(dense_max, ("seq", "sub"))
    lift = jnp.exp(dense_max - top)
    total_sum, total_out = (
        gathered_total(lift * dense_sum, ("seq", "sub")),
        gathered_total(lift[..., None] * dense_out, ("seq", "sub")),
    )
    denominator = lax.dynamic_slice_in_dim(total_sum, head_start, own_heads, 1)
    summed = lax.dynamic_slice_in_dim(total_out, head_start, own_heads, 1)
    return (summed / denominator[..., None]).astype(jnp.bfloat16)


def solution(mesh):
    return jax.shard_map(
        shards,
        mesh=mesh,
        in_specs=(
            P(("group", "sub"), "head", None),
            P(("group", "sub")),
            P(("group", "seq", "sub"), "head", None),
            P(("group", "seq", "sub"), "head", None),
        ),
        out_specs=P("group", ("head", "sub"), None),
        check_vma=False,
    )
```

profile of v0, /device:TPU:38, one launch (start us, length us, event | category | flops | bytes accessed | tf_op | source)
XLA Modules:
  0.0 254.9 jit_solution(14770276685209247385)
XLA Ops:
  6.6 1.4 broadcast_in_dim.56
  7.9 3.2 %all-to-all-start = ((s32[2,1,8]{2,1,0:T(1,128)}), s32[2,1,8]{2,1,0:T(1,128)S(1)}, u32[]{:S(2)}, u32[]{:S(2)}) async-start(s32[2,1,8]{2,1,0:T(1,128)} %broadcast_in_dim.56), calls=%async_computation | async-start | bytes 2048 | tf_op jit(solution)/shard_map/all_to_all | solution.py:22
  11.2 1.2 all-to-all-done
  12.4 1.3 broadcast_in_dim.59
  13.7 3.3 %all-to-all-start.1 = ((bf16[2,8,8,128]{3,2,1,0:T(8,128)(2,1)}), bf16[2,8,8,128]{3,2,1,0:T(8,128)(2,1)S(1)}, u32[]{:S(2)}, u32[]{:S(2)}) async-start(bf16[2,8,8,128]{3,2,1,0:T(8,128)(2,1)} %broadcast_in_dim.59), calls=%async_computation.1 | async-start | bytes 65536 | tf_op jit(solution)/shard_map/all_to_all | solution.py:22
  17.1 0.5 broadcast.104
  17.6 0.7 reduce.7
  18.4 0.1 reduce.2
  18.8 0.6 gather_fusion
  19.4 1.3 fusion.28
  20.8 0.1 select_reduce_fusion
  21.0 0.6 gather_fusion.1
  21.6 0.3 fusion.14
  21.9 96.2 %pmax.14 = f32[16,8]{0,1:T(8,128)S(1)} all-reduce(f32[16,8]{0,1:T(8,128)S(1)} %bitcast.33), channel_id=1, replica_groups=mesh['group'=2,'seq'=32,'head'=4,'sub'=2] {'seq'}, use_global_device_ids=true, to_apply=%region_4.5 | all-reduce | flops 128 | bytes 1024 | tf_op jit(solution)/shard_map/pmax | solution.py:30
  118.1 2.5 pmax.15
  120.6 0.1 fusion.27
  120.7 2.3 fusion.7
  123.0 0.2 fusion.12
  123.3 0.7 copy_multiply_fusion
  124.2 0.1 fusion.11
  124.3 53.0 %all-gather.1 = f32[64,16,8]{1,2,0:T(8,128)S(1)} all-gather(f32[1,16,8]{1,2,0:T(8,128)S(1)} %fusion.11), channel_id=2, replica_groups=mesh['group'=2,'seq'=32,'head'=4,'sub'=2] {'seq','sub'}, dimensions={0}, use_global_device_ids=true | all-gather | bytes 33280 | tf_op jit(solution)/shard_map/all_gather | solution.py:34
  177.3 67.5 %all-gather.4.cloned.1.call-done = f32[64,16,8,128]{3,2,1,0:T(8,128)} async-done(((f32[1,16,8,128]{3,2,1,0:T(8,128)}), f32[64,16,8,128]{3,2,1,0:T(8,128)}) %all-gather.4.cloned.1.call-update) | async-done | bytes 4194320 | tf_op jit(solution)/shard_map/all_gather | solution.py:34
  244.9 2.4 reduce_sum.37
  247.4 0.6 copy.37
  (25 shorter events, 1.0 us)
Async XLA Ops:
  6.5 12.8 %copy-start = (bf16[4096,2,128]{2,1,0:T(2,128)(2,1)S(1)}, bf16[4096,2,128]{2,1,0:T(2,128)(2,1)}, u32[]{:S(2)}) copy-start(bf16[4096,2,128]{2,1,0:T(2,128)(2,1)} %param.6) | copy-start | bytes 6291460
  7.9 4.5 %all-to-all-start = ((s32[2,1,8]{2,1,0:T(1,128)}), s32[2,1,8]{2,1,0:T(1,128)S(1)}, u32[]{:S(2)}, u32[]{:S(2)}) async-start(s32[2,1,8]{2,1,0:T(1,128)} %broadcast_in_dim.56), calls=%async_computation | async-start | bytes 2048 | tf_op jit(solution)/shard_map/all_to_all | solution.py:22
  13.7 5.0 %all-to-all-start.1 = ((bf16[2,8,8,128]{3,2,1,0:T(8,128)(2,1)}), bf16[2,8,8,128]{3,2,1,0:T(8,128)(2,1)S(1)}, u32[]{:S(2)}, u32[]{:S(2)}) async-start(bf16[2,8,8,128]{3,2,1,0:T(8,128)(2,1)} %broadcast_in_dim.59), calls=%async_computation.1 | async-start | bytes 65536 | tf_op jit(solution)/shard_map/all_to_all | solution.py:22
  17.0 227.8 %all-gather.4.cloned.1.call-start = ((), (), s32[]{:S(2)}) async-start(), calls=%async_computation.2 | async-start | bytes 4259840 | tf_op jit(solution)/shard_map/all_gather | solution.py:34
Sparse Core Ops, SparseCore 0:
  124.2 120.6 all-gather.3
where the time goes:
time: 257 us; the launch traced here: 255 us
  blocking collectives  152 us (59%)
  waiting for transfers between devices  68.8 us (27%)
  between operations  13.6 us (5%)
  starting transfers between devices  6.57 us (3%)
  local copies, waits for them, and re-layouts  5.56 us (2%)
  other arithmetic  4.74 us (2%)
  matrix products  3.94 us (2%)
    pmax x2, blocking collectives, one_axis_at_a_time(): return functools.reduce(lax.pmax, axes, x)  98.7 us
    all_gather x1, waiting for transfers between devices, gathered_total(): pieces = lax.all_gather(x, axis)  67.5 us
    all_gather x1, blocking collectives, gathered_total(): pieces = lax.all_gather(x, axis)  53 us
    all_to_all x2, starting transfers between devices, sent_to_all(): return lax.all_to_all(copies, axis, split_axis=0, concat_axis=0, tiled=True)  6.51 us
  transfers between devices with their start and end apart: 3, of which 2 were waited for; matrix products, arithmetic and copies ran while one was open for 1% of the time, Pallas kernels for 0%

commit v1 on v0

v1 whole, which is shorter than its diff:
```python
import functools

import jax
import jax.numpy as jnp
from jax import lax
from jax.experimental import pallas as pl
from jax.experimental.pallas import tpu as pltpu
from jax.sharding import PartitionSpec as P

PAGE = 128
LONGEST = 192
CORES = 2
NEG = -1e30
MESH = pl.DeviceIdType.MESH
PARTS = 4


def kernel(
    chips,
    q_hbm,
    len_hbm,
    k_hbm,
    v_hbm,
    out_ref,
    kbuf,
    vbuf,
    qbuf,
    score,
    weight,
    run_max,
    run_sum,
    run_out,
    sent,
    got,
    final,
    len_vm,
    len_sm,
    start_sm,
    k_sem,
    v_sem,
    in_sem,
    x_send,
    x_recv,
    token,
    r_send,
    r_recv,
    g_send,
    g_recv,
):
    c, s = lax.axis_index("seq"), lax.axis_index("sub")
    own_requests, heads, width = q_hbm.shape
    requests = own_requests * CORES
    group = heads // CORES
    rows = kbuf.shape[0]
    pages = rows // (PAGE * CORES)
    page_rows = PAGE * CORES
    chunks = k_sem.shape[0]
    chunk_rows = rows // chunks
    chunk_pages = pages // chunks
    per_part = requests // PARTS
    reach = got.shape[0] // (2 * CORES)
    far = chips // 4

    def chip(offset):
        return lax.rem(c + (offset + chips), chips)

    def at(offset, core):
        return {"seq": chip(offset), "sub": core}

    barrier = pltpu.get_barrier_semaphore()
    near = [(o, k) for o in (1, -1) for k in range(CORES)]
    for o, k in near:
        pl.semaphore_signal(barrier, inc=1, device_id=at(o, k), device_id_type=MESH)
    pl.semaphore_signal(barrier, inc=1, device_id=at(0, 1 - s), device_id_type=MESH)

    def k_copy(i):
        part = pl.ds(i * chunk_rows, chunk_rows)
        return pltpu.make_async_copy(k_hbm.at[part], kbuf.at[part], k_sem.at[i])

    def v_copy(i):
        part = pl.ds(i * chunk_rows, chunk_rows)
        return pltpu.make_async_copy(v_hbm.at[part], vbuf.at[part], v_sem.at[i])

    own = pl.ds(s * own_requests, own_requests)
    q_own = pltpu.make_async_copy(q_hbm, qbuf.at[own], in_sem.at[0])
    l_own = pltpu.make_async_copy(len_hbm, len_vm.at[s], in_sem.at[1])
    q_own.start()
    l_own.start()
    for i in range(chunks):
        k_copy(i).start()
    for i in range(chunks):
        v_copy(i).start()

    pl.semaphore_wait(barrier, len(near) + 1)
    q_away = pltpu.make_async_remote_copy(
        src_ref=q_hbm, dst_ref=qbuf.at[own], send_sem=x_send.at[0], recv_sem=x_recv.at[0],
        device_id=at(0, 1 - s), device_id_type=MESH,
    )
    l_away = pltpu.make_async_remote_copy(
        src_ref=len_hbm, dst_ref=len_vm.at[s], send_sem=x_send.at[1], recv_sem=x_recv.at[1],
        device_id=at(0, 1 - s), device_id_type=MESH,
    )
    l_away.start()
    q_away.start()

    def signal_level(level):
        for side, o in enumerate((1 << level, -(1 << level))):
            pl.semaphore_signal(token.at[level, side], inc=1, device_id=at(o, s), device_id_type=MESH)

    def wait_level(level):
        for side in range(2):
            pl.semaphore_wait(token.at[level, side], 1)

    signal_level(0)

    l_own.wait()
    l_away.wait()
    l_down = pltpu.make_async_copy(len_vm, len_sm, in_sem.at[2])
    l_down.start()
    l_down.wait()
    starts = []
    total = jnp.int32(0)
    for r in range(requests):
        starts.append(total)
        start_sm[r] = total
        total = total + len_sm[r // own_requests, r % own_requests]
    start_sm[requests] = total
    base = (c * CORES + s) * pages
    owner = jnp.int32(-1)
    for r in range(requests):
        owner = owner + (starts[r] <= base).astype(jnp.int32)
    owners, firsts = [owner], [None]
    for p in range(1, pages):
        begins = start_sm[owner + 1] <= base + p
        owner = jnp.minimum(owner + begins.astype(jnp.int32), requests - 1)
        owners.append(owner)
        firsts.append(begins)

    q_own.wait()
    q_away.wait()
    lane_head = lax.rem(lax.broadcasted_iota(jnp.int32, (heads, page_rows), 1), CORES)
    row_head = lax.broadcasted_iota(jnp.int32, (heads, page_rows), 0) // group
    mine = lane_head == row_head
    scale = float(width) ** -0.5
    running = None
    for p in range(pages):
        if p % chunk_pages == 0:
            k_copy(p // chunk_pages).wait()
        keys = kbuf[p * page_rows : (p + 1) * page_rows, :]
        values = lax.dot_general(
            qbuf[owners[p]], keys, (((1,), (1,)), ((), ())), preferred_element_type=jnp.float32
        )
        values = jnp.where(mine, values * scale, NEG)
        score[p] = values
        top = jnp.broadcast_to(jnp.max(values, axis=1, keepdims=True), (heads, width))
        running = top if p == 0 else jnp.where(firsts[p], top, jnp.maximum(running, top))
        run_max[p] = running

    wait_level(0)
    signal_level(1)

    running = None
    for p in range(pages):
        last = jnp.clip(start_sm[owners[p] + 1] - base - 1, 0, pages - 1)
        peak = run_max[last].astype(jnp.bfloat16).astype(jnp.float32)
        half = jnp.exp(score[p] - jnp.concatenate([peak] * CORES, axis=1)).astype(jnp.bfloat16)
        weight[p] = half
        added = jnp.broadcast_to(
            jnp.sum(half.astype(jnp.float32), axis=1, keepdims=True), (heads, width)
        )
        running = added if p == 0 else jnp.where(firsts[p], added, running + added)
        run_sum[p] = running

    running = None
    for p in range(pages):
        if p % chunk_pages == 0:
            v_copy(p // chunk_pages).wait()
        values = vbuf[p * page_rows : (p + 1) * page_rows, :]
        added = jnp.dot(weight[p], values, preferred_element_type=jnp.float32)
        running = added if p == 0 else jnp.where(firsts[p], added, running + added)
        run_out[p] = running

    lane = lax.broadcasted_iota(jnp.int32, (heads, width), 1)
    tops, sums, outs = [], [], []
    for r in range(requests):
        begin = jnp.maximum(starts[r] - base, 0)
        end = jnp.minimum(start_sm[r + 1] - base, pages)
        here = end > begin
        last = jnp.clip(end - 1, 0, pages - 1)
        peak = jnp.where(here, run_max[last], NEG).astype(jnp.bfloat16).astype(jnp.float32)
        weights = jnp.where(here, run_sum[last], 0.0)
        high = weights.astype(jnp.bfloat16).astype(jnp.float32)
        tops.append(jnp.where(lane < 32, peak, jnp.where(lane < 64, high, weights - high)))
        outs.append(jnp.where(here, run_out[last], 0.0))

    for j in range(PARTS):
        members = range(j * per_part, (j + 1) * per_part)
        for k in range(CORES):
            cut = slice(k * group, (k + 1) * group)
            numbers = jnp.concatenate([outs[r][cut] for r in members], axis=0)
            stats = jnp.concatenate([tops[r][cut] for r in members], axis=0)
            sent[j, k] = jnp.concatenate([numbers, stats], axis=0).astype(jnp.bfloat16)

    wait_level(1)
    signal_level(2)

    part_rows = per_part * group
    offsets = [o for n in range(reach, 0, -1) for o in (n, -n)] + [0]

    def part_copy(o, k, n):
        return pltpu.make_async_remote_copy(
            src_ref=sent.at[lax.rem(chip(o), PARTS), k],
            dst_ref=got.at[(reach - o) * CORES + s],
            send_sem=r_send.at[n],
            recv_sem=r_recv.at[(reach - o) * CORES + s],
            device_id=at(o, k),
            device_id_type=MESH,
        )

    def part_arrival(o, k):
        slot = (reach + o) * CORES + k
        return pltpu.make_async_remote_copy(
            src_ref=sent.at[0, 0], dst_ref=got.at[slot], send_sem=r_send.at[0], recv_sem=r_recv.at[slot],
            device_id=at(0, 1 - s), device_id_type=MESH,
        )

    part_copies = []
    for o in offsets:
        for k in range(CORES) if o else (1 - s,):
            part_copies.append(part_copy(o, k, len(part_copies)))
            part_copies[-1].start()
    got[reach * CORES + s] = sent[lax.rem(c, PARTS), s]
    for o in offsets:
        for k in range(CORES) if o else (1 - s,):
            part_arrival(o, k).wait_recv()

    slots = got.shape[0]
    stats = [got[i, part_rows:, :].astype(jnp.float32) for i in range(slots)]
    peak = functools.reduce(jnp.maximum, stats)
    numer, denom = 0.0, 0.0
    for i in range(slots):
        lift = jnp.exp(stats[i][:, 0:1] - peak[:, 0:1])
        numer = numer + lift * got[i, :part_rows, :].astype(jnp.float32)
        denom = denom + lift * stats[i]
    denom = denom[:, 32:33] + denom[:, 64:65]
    denom = jnp.where(denom > 0.0, denom, 1.0)
    final[c] = (numer / denom).astype(jnp.bfloat16)

    spread = []

    def pass_on(origin, o):
        cp = pltpu.make_async_remote_copy(
            src_ref=final.at[origin], dst_ref=final.at[origin], send_sem=g_send.at[len(spread)],
            recv_sem=g_recv.at[origin], device_id=at(o, s), device_id_type=MESH,
        )
        spread.append((origin, o))
        cp.start()

    def spread_copy(n, origin, o):
        return pltpu.make_async_remote_copy(
            src_ref=final.at[origin], dst_ref=final.at[origin], send_sem=g_send.at[n],
            recv_sem=g_recv.at[origin], device_id=at(o, s), device_id_type=MESH,
        )

    known = 1 << 2
    for n in range(1, known + 1):
        for o in (n, -n):
            pass_on(c, o)
    wait_level(2)
    for n in range(known + 1, far + 1):
        for o in (n, -n):
            pass_on(c, o)

    direct = len(spread)

    def upward():
        below = chip(-far)
        spread_copy(0, below, 1).wait_recv()
        for n in range(1, far + 1):
            spread_copy(direct + n - 1, below, n).start()

    def downward():
        above = chip(far)
        spread_copy(0, above, 1).wait_recv()
        for n in range(1, far):
            spread_copy(direct + far + n - 1, above, -n).start()

    @pl.when(c < chips // 2)
    def _():
        downward()
        upward()

    @pl.when(c >= chips // 2)
    def _():
        upward()
        downward()

    for n in range(1, chips):
        if n not in (far, chips - far):
            spread_copy(0, chip(n), 1).wait_recv()

    row_request = lax.broadcasted_iota(jnp.int32, (part_rows, width), 0) // group
    for j in range(PARTS):
        block = None
        for i in range(per_part):
            home = starts[j * per_part + i] // (pages * CORES)
            home = home + lax.rem(j - lax.rem(home, PARTS) + PARTS, PARTS)
            piece = final[lax.rem(home, chips)].astype(jnp.float32)
            block = piece if i == 0 else jnp.where(row_request == i, piece, block)
        out_ref[j * part_rows : (j + 1) * part_rows, :] = block.astype(jnp.bfloat16)

    for n in range(len(part_copies)):
        part_copies[n].wait_send()
    for n, (origin, o) in enumerate(spread):
        spread_copy(n, origin, o).wait_send()
    for n in range(1, far + 1):
        spread_copy(direct + n - 1, chip(-far), n).wait_send()
    for n in range(1, far):
        spread_copy(direct + far + n - 1, chip(far), -n).wait_send()


def shards(queries, lengths, k_cache, v_cache):
    chips = lax.axis_size("seq")
    own_requests, heads, width = queries.shape
    tokens, key_heads, _ = k_cache.shape
    requests = own_requests * CORES
    group = heads // key_heads
    rows = tokens * key_heads
    pages = tokens // PAGE
    page_rows = PAGE * key_heads
    span = -(-(LONGEST - 1) // (pages * CORES))
    window = 2 * span + 1
    part_rows = requests // PARTS * group
    chunks = 4
    far = chips // 4
    bf16, f32 = jnp.bfloat16, jnp.float32
    result = pl.pallas_call(
        functools.partial(kernel, chips),
        out_shape=jax.ShapeDtypeStruct((requests * group, width), bf16),
        in_specs=[pl.BlockSpec(memory_space=pl.ANY)] * 4,
        out_specs=pl.BlockSpec(memory_space=pltpu.VMEM),
        scratch_shapes=[
            pltpu.VMEM((rows, width), bf16),
            pltpu.VMEM((rows, width), bf16),
            pltpu.VMEM((requests, heads, width), bf16),
            pltpu.VMEM((pages, heads, page_rows), f32),
            pltpu.VMEM((pages, heads, page_rows), bf16),
            pltpu.VMEM((pages, heads, width), f32),
            pltpu.VMEM((pages, heads, width), f32),
            pltpu.VMEM((pages, heads, width), f32),
            pltpu.VMEM((PARTS, CORES, 2 * part_rows, width), bf16),
            pltpu.VMEM((window * CORES, 2 * part_rows, width), bf16),
            pltpu.VMEM((chips, part_rows, width), bf16),
            pltpu.VMEM((CORES, own_requests), jnp.int32),
            pltpu.SMEM((CORES, own_requests), jnp.int32),
            pltpu.SMEM((requests + 1,), jnp.int32),
            pltpu.SemaphoreType.DMA((chunks,)),
            pltpu.SemaphoreType.DMA((chunks,)),
            pltpu.SemaphoreType.DMA((3,)),
            pltpu.SemaphoreType.DMA((2,)),
            pltpu.SemaphoreType.DMA((2,)),
            pltpu.SemaphoreType.REGULAR((3, 2)),
            pltpu.SemaphoreType.DMA((window * CORES,)),
            pltpu.SemaphoreType.DMA((window * CORES,)),
            pltpu.SemaphoreType.DMA((4 * far,)),
            pltpu.SemaphoreType.DMA((chips,)),
        ],
        compiler_params=pltpu.CompilerParams(collective_id=0, has_side_effects=True),
    )(queries, lengths, k_cache.reshape(rows, width), v_cache.reshape(rows, width))
    return result.reshape(requests, group, width)


def solution(mesh):
    return jax.shard_map(
        shards,
        mesh=mesh,
        in_specs=(
            P(("group", "sub"), "head", None),
            P(("group", "sub")),
            P(("group", "seq", "sub"), "head", None),
            P(("group", "seq", "sub"), "head", None),
        ),
        out_specs=P("group", ("head", "sub"), None),
        check_vma=False,
    )
```

time: 257 us -> 68.8 us (0.27)
  blocking collectives: 152 us -> 0 us
  waiting for transfers between devices: 68.8 us -> 0 us
  Pallas kernels: 0 us -> 67.2 us
  between operations: 13.6 us -> 0.01 us
  starting transfers between devices: 6.57 us -> 0 us
  other arithmetic: 4.74 us -> 0 us
  local copies, waits for them, and re-layouts: 5.56 us -> 1.33 us
  matrix products: 3.94 us -> 0 us
    pmax x2 -> x0, blocking collectives: 98.7 us -> none  [one_axis_at_a_time(): return functools.reduce(lax.pmax, axes, x)]
    all_gather x1 -> x0, waiting for transfers between devices: 67.5 us -> none  [gathered_total(): pieces = lax.all_gather(x, axis)]
    pallas_call x0 -> x1, Pallas kernels: none -> 67.2 us  [shards(): pl.pallas_call(functools.partial(kernel, chips), out_shape=jax.ShapeDtype...]
    all_gather x1 -> x0, blocking collectives: 53 us -> none  [gathered_total(): pieces = lax.all_gather(x, axis)]
    all_to_all x2 -> x0, starting transfers between devices: 6.51 us -> none  [sent_to_all(): return lax.all_to_all(copies, axis, split_axis=0, concat_axis=0, tiled=True)]
    dot_general x3 -> x0, matrix products: 3.82 us -> none  [the longest x1 2.29 us: shards(): jnp.einsum('pkgs,pskd->pkgd', weights.astype(jnp.bfloat16), value_pages,...]
    reduce_sum x4 -> x0, other arithmetic: 2.85 us -> none  [the longest x2 2.48 us: gathered_total(): return pieces.sum(axis=0)]
    broadcast_in_dim x2 -> x0, local copies, waits for them, and re-layouts: 2.69 us -> none  [sent_to_all(): copies = jnp.broadcast_to(x, (lax.axis_size(axis), *x.shape))]
  transfers between devices with their start and end apart: 3 -> 0, of which waited for: 2 -> 0; matrix products, arithmetic and copies ran while one was open for 1% -> 0% of each run, Pallas kernels for 0% -> 0%
where the time goes in v1:
time: 68.8 us; the launch traced here: 68.6 us
  Pallas kernels  67.2 us (98%)
  local copies, waits for them, and re-layouts  1.33 us (2%)
    pallas_call x1, Pallas kernels, shards(): pl.pallas_call(functools.partial(kernel, chips), out_shape=jax.ShapeDtype...  67.2 us

profile of v1, /device:TPU:38, one launch (start us, length us, event | category | flops | bytes accessed | tf_op | source)
XLA Modules:
  0.0 68.6 jit_solution(8475740974413265840)
XLA Ops:
  0.0 67.2 %shard_map.46 = bf16[64,128]{1,0:T(8,128)(2,1)} custom-call(bf16[8,8,128]{2,1,0:T(8,128)(2,1)} %q_hbm.1, s32[8]{0:T(128)} %len_hbm.1, bf16[8192,128]{1,0:T(8,128)(2,1)} %bitcast.3, bf16[8192,128]{1,0:T(8,128)(2,1)} %bitcast.4), custom_call_target="tpu_custom_call" | custom-call | tf_op jit(solution)/shard_map/pallas_call | solution.py:337
  67.2 1.3 %copy.6 = bf16[16,4,128]{2,1,0:T(4,128)(2,1)} copy(bf16[16,4,128]{2,1,0:T(4,128)(2,1)} %bitcast.5) | data formatting | bytes 32768

commit v2 on v1

v2 whole, which is shorter than its diff:
```python
import functools

import jax
import jax.numpy as jnp
from jax import lax
from jax.experimental import pallas as pl
from jax.experimental.pallas import tpu as pltpu
from jax.sharding import PartitionSpec as P

PAGE = 128
LONGEST = 192
CORES = 2
NEG = -1e30
MESH = pl.DeviceIdType.MESH
STEPS = (1, 2, 4, 4)
PARTS = 4


def rounded(x):
    return x.astype(jnp.bfloat16).astype(jnp.float32)


def kernel(
    chips,
    q_hbm,
    len_hbm,
    k_hbm,
    v_hbm,
    out_ref,
    kbuf,
    vbuf,
    qbuf,
    weight,
    page_max,
    page_sum,
    run_max,
    run_sum,
    run_out,
    sent,
    got,
    final,
    len_vm,
    len_sm,
    start_sm,
    k_sem,
    v_sem,
    in_sem,
    x_send,
    x_recv,
    token,
    r_send,
    r_recv,
    g_send,
    h_send,
    g_recv,
):
    c, s = lax.axis_index("seq"), lax.axis_index("sub")
    own_requests, heads, width = q_hbm.shape
    requests = own_requests * CORES
    group = heads // CORES
    rows = kbuf.shape[0]
    pages = rows // (PAGE * CORES)
    page_rows = PAGE * CORES
    chunks = k_sem.shape[0]
    chunk_rows = rows // chunks
    chunk_pages = pages // chunks
    per_part = requests // PARTS
    reach = got.shape[0] // (2 * CORES)
    far = sum(STEPS) + 1

    def chip(offset):
        return lax.rem(c + (offset + chips), chips)

    def at(offset, core):
        return {"seq": chip(offset), "sub": core}

    barrier = pltpu.get_barrier_semaphore()
    near = [(o, k) for o in (1, -1) for k in range(CORES)]
    for o, k in near:
        pl.semaphore_signal(barrier, inc=1, device_id=at(o, k), device_id_type=MESH)
    pl.semaphore_signal(barrier, inc=1, device_id=at(0, 1 - s), device_id_type=MESH)

    def k_copy(i):
        part = pl.ds(i * chunk_rows, chunk_rows)
        return pltpu.make_async_copy(k_hbm.at[part], kbuf.at[part], k_sem.at[i])

    def v_copy(i):
        part = pl.ds(i * chunk_rows, chunk_rows)
        return pltpu.make_async_copy(v_hbm.at[part], vbuf.at[part], v_sem.at[i])

    own = pl.ds(s * own_requests, own_requests)
    l_out = pltpu.make_async_copy(len_hbm, len_vm, in_sem.at[2])
    l_own = pltpu.make_async_copy(len_hbm, len_sm.at[s], in_sem.at[1])
    q_own = pltpu.make_async_copy(q_hbm, qbuf.at[own], in_sem.at[0])
    l_out.start()
    q_own.start()
    l_own.start()
    for i in range(chunks):
        k_copy(i).start()
    l_out.wait()
    q_own.wait()
    pl.semaphore_wait(barrier, len(near) + 1)
    l_away = pltpu.make_async_remote_copy(
        src_ref=len_vm, dst_ref=len_sm.at[s], send_sem=x_send.at[1], recv_sem=x_recv.at[1],
        device_id=at(0, 1 - s), device_id_type=MESH,
    )
    q_away = pltpu.make_async_remote_copy(
        src_ref=qbuf.at[own], dst_ref=qbuf.at[own], send_sem=x_send.at[0], recv_sem=x_recv.at[0],
        device_id=at(0, 1 - s), device_id_type=MESH,
    )
    l_away.start()
    q_away.start()
    for i in range(chunks):
        v_copy(i).start()

    def signal_level(level):
        for side, o in enumerate((STEPS[level], -STEPS[level])):
            pl.semaphore_signal(token.at[level, side], inc=1, device_id=at(o, s), device_id_type=MESH)

    def wait_level(level):
        for side in range(2):
            pl.semaphore_wait(token.at[level, side], 1)

    signal_level(0)

    l_own.wait()
    l_away.wait()
    starts = []
    total = jnp.int32(0)
    for r in range(requests):
        starts.append(total)
        start_sm[r] = total
        total = total + len_sm[r // own_requests, r % own_requests]
    start_sm[requests] = total
    base = (c * CORES + s) * pages
    owner = jnp.int32(-1)
    for r in range(requests):
        owner = owner + (starts[r] <= base).astype(jnp.int32)
    owners, firsts = [owner], [None]
    for p in range(1, pages):
        begins = start_sm[owner + 1] <= base + p
        owner = jnp.minimum(owner + begins.astype(jnp.int32), requests - 1)
        owners.append(owner)
        firsts.append(begins)

    q_away.wait()
    lane_head = lax.rem(lax.broadcasted_iota(jnp.int32, (heads, page_rows), 1), CORES)
    row_head = lax.broadcasted_iota(jnp.int32, (heads, page_rows), 0) // group
    mine = lane_head == row_head
    scale = float(width) ** -0.5
    running = None
    for p in range(pages):
        if p % chunk_pages == 0:
            k_copy(p // chunk_pages).wait()
        keys = kbuf[p * page_rows : (p + 1) * page_rows, :]
        values = lax.dot_general(
            qbuf[owners[p]], keys, (((1,), (1,)), ((), ())), preferred_element_type=jnp.float32
        )
        values = jnp.where(mine, values * scale, NEG)
        top = jnp.broadcast_to(jnp.max(values, axis=1, keepdims=True), (heads, width))
        values = jnp.exp(values - jnp.concatenate([top] * CORES, axis=1))
        weight[p] = values.astype(jnp.bfloat16)
        page_max[p] = top
        page_sum[p] = jnp.broadcast_to(jnp.sum(values, axis=1, keepdims=True), (heads, width))
        running = top if p == 0 else jnp.where(firsts[p], top, jnp.maximum(running, top))
        run_max[p] = running

    wait_level(0)
    signal_level(1)

    summed = gathered = None
    for p in range(pages):
        if p % chunk_pages == 0:
            v_copy(p // chunk_pages).wait()
        last = jnp.clip(start_sm[owners[p] + 1] - base - 1, 0, pages - 1)
        lift = jnp.exp(page_max[p] - rounded(run_max[last]))
        values = vbuf[p * page_rows : (p + 1) * page_rows, :]
        added = lift * jnp.dot(weight[p], values, preferred_element_type=jnp.float32)
        gathered = added if p == 0 else jnp.where(firsts[p], added, gathered + added)
        run_out[p] = gathered
        added = lift * page_sum[p]
        summed = added if p == 0 else jnp.where(firsts[p], added, summed + added)
        run_sum[p] = summed

    lane = lax.broadcasted_iota(jnp.int32, (heads, width), 1)
    half = lax.rem(lane, width // 2)
    tops, sums, outs = [], [], []
    for r in range(requests):
        begin = jnp.maximum(starts[r] - base, 0)
        end = jnp.minimum(start_sm[r + 1] - base, pages)
        here = end > begin
        last = jnp.clip(end - 1, 0, pages - 1)
        peak = rounded(jnp.where(here, run_max[last], NEG))
        weights = jnp.where(here, run_sum[last], 0.0)
        high = weights.astype(jnp.bfloat16).astype(jnp.float32)
        tops.append(jnp.where(half < 16, peak, jnp.where(half < 32, high, weights - high)))
        outs.append(jnp.where(here, run_out[last], 0.0))

    for j in range(PARTS):
        members = range(j * per_part, (j + 1) * per_part)
        for k in range(CORES):
            cut = slice(k * group, (k + 1) * group)
            numbers = jnp.concatenate([outs[r][cut] for r in members], axis=0)
            lower, upper = (
                jnp.concatenate([tops[r][cut] for r in some], axis=0)
                for some in (members[: per_part // 2], members[per_part // 2 :])
            )
            stats = jnp.where(lane < width // 2, lower, upper)
            sent[j, k] = jnp.concatenate([numbers, stats], axis=0).astype(jnp.bfloat16)

    wait_level(1)
    signal_level(2)

    part_rows = per_part * group
    offsets = [o for n in range(reach, 0, -1) for o in (n, -n)] + [0]

    def part_copy(o, k, n):
        return pltpu.make_async_remote_copy(
            src_ref=sent.at[lax.rem(chip(o), PARTS), k],
            dst_ref=got.at[(reach - o) * CORES + s],
            send_sem=r_send.at[n],
            recv_sem=r_recv.at[(reach - o) * CORES + s],
            device_id=at(o, k),
            device_id_type=MESH,
        )

    def part_arrival(o, k):
        slot = (reach + o) * CORES + k
        return pltpu.make_async_remote_copy(
            src_ref=sent.at[0, 0], dst_ref=got.at[slot], send_sem=r_send.at[0], recv_sem=r_recv.at[slot],
            device_id=at(0, 1 - s), device_id_type=MESH,
        )

    part_copies = []
    for o in offsets:
        for k in range(CORES) if o else (1 - s,):
            part_copies.append(part_copy(o, k, len(part_copies)))
            part_copies[-1].start()
    got[reach * CORES + s] = sent[lax.rem(c, PARTS), s]
    wait_level(2)
    signal_level(3)
    for o in offsets:
        for k in range(CORES) if o else (1 - s,):
            part_arrival(o, k).wait_recv()

    slots = got.shape[0]
    stats = [got[i, part_rows:, :].astype(jnp.float32) for i in range(slots)]
    peak = functools.reduce(jnp.maximum, stats)
    blocks = []
    for t in range(2):
        first = t * width // 2
        numer, denom = 0.0, 0.0
        for i in range(slots):
            lift = jnp.exp(stats[i][:, first : first + 1] - peak[:, first : first + 1])
            part = got[i, t * part_rows // 2 : (t + 1) * part_rows // 2, :]
            numer = numer + lift * part.astype(jnp.float32)
            denom = denom + lift * stats[i]
        denom = denom[:, first + 16 : first + 17] + denom[:, first + 32 : first + 33]
        blocks.append(numer / jnp.where(denom > 0.0, denom, 1.0))
    final[c] = jnp.concatenate(blocks, axis=0).astype(jnp.bfloat16)

    def spread_copy(sem, origin, to):
        return pltpu.make_async_remote_copy(
            src_ref=final.at[origin], dst_ref=final.at[origin], send_sem=sem,
            recv_sem=g_recv.at[origin], device_id={"seq": to, "sub": s}, device_id_type=MESH,
        )

    def arrived(origin):
        spread_copy(g_send.at[0], origin, chip(1)).wait_recv()

    wait_level(3)
    beyond = chips // 2 - far
    direct = [o for n in range(1, far + 1) for o in (n, -n)]
    for to in range(chips):
        ahead = lax.rem(to - c + chips, chips)

        @pl.when((ahead > 0) & ((ahead <= far) | (ahead >= chips - far)))
        def _():
            spread_copy(g_send.at[to], c, to).start()

    def upward(act):
        for n in range(1, beyond + 1):
            act(spread_copy(h_send.at[n - 1], chip(-far), chip(n)))

    def downward(act):
        for n in range(1, beyond):
            act(spread_copy(h_send.at[beyond + n - 1], chip(far), chip(-n)))

    @pl.when(c < chips // 2)
    def _():
        arrived(chip(far))
        downward(lambda copy: copy.start())
        arrived(chip(-far))
        upward(lambda copy: copy.start())

    @pl.when(c >= chips // 2)
    def _():
        arrived(chip(-far))
        upward(lambda copy: copy.start())
        arrived(chip(far))
        downward(lambda copy: copy.start())

    for n in range(1, chips):
        if n not in (far, chips - far):
            arrived(chip(n))

    row_request = lax.broadcasted_iota(jnp.int32, (part_rows, width), 0) // group
    for j in range(PARTS):
        block = None
        for i in range(per_part):
            home = starts[j * per_part + i] // (pages * CORES)
            home = home + lax.rem(j - lax.rem(home, PARTS) + PARTS, PARTS)
            piece = final[lax.rem(home, chips)].astype(jnp.float32)
            block = piece if i == 0 else jnp.where(row_request == i, piece, block)
        out_ref[j * part_rows : (j + 1) * part_rows, :] = block.astype(jnp.bfloat16)

    for n in range(len(part_copies)):
        part_copies[n].wait_send()
    for o in direct:
        spread_copy(g_send.at[chip(o)], c, chip(o)).wait_send()
    upward(lambda copy: copy.wait_send())
    downward(lambda copy: copy.wait_send())


def shards(queries, lengths, k_cache, v_cache):
    chips = lax.axis_size("seq")
    own_requests, heads, width = queries.shape
    tokens, key_heads, _ = k_cache.shape
    requests = own_requests * CORES
    group = heads // key_heads
    rows = tokens * key_heads
    pages = tokens // PAGE
    page_rows = PAGE * key_heads
    span = -(-(LONGEST - 1) // (pages * CORES))
    window = 2 * span + 1
    part_rows = requests // PARTS * group
    chunks = 4
    bf16, f32 = jnp.bfloat16, jnp.float32
    result = pl.pallas_call(
        functools.partial(kernel, chips),
        out_shape=jax.ShapeDtypeStruct((requests * group, width), bf16),
        in_specs=[pl.BlockSpec(memory_space=pl.ANY)] * 4,
        out_specs=pl.BlockSpec(memory_space=pltpu.VMEM),
        scratch_shapes=[
            pltpu.VMEM((rows, width), bf16),
            pltpu.VMEM((rows, width), bf16),
            pltpu.VMEM((requests, heads, width), bf16),
            pltpu.VMEM((pages, heads, page_rows), bf16),
            pltpu.VMEM((pages, heads, width), f32),
            pltpu.VMEM((pages, heads, width), f32),
            pltpu.VMEM((pages, heads, width), f32),
            pltpu.VMEM((pages, heads, width), f32),
            pltpu.VMEM((pages, heads, width), f32),
            pltpu.VMEM((PARTS, CORES, part_rows * 3 // 2, width), bf16),
            pltpu.VMEM((window * CORES, part_rows * 3 // 2, width), bf16),
            pltpu.VMEM((chips, part_rows, width), bf16),
            pltpu.VMEM((own_requests,), jnp.int32),
            pltpu.SMEM((CORES, own_requests), jnp.int32),
            pltpu.SMEM((requests + 1,), jnp.int32),
            pltpu.SemaphoreType.DMA((chunks,)),
            pltpu.SemaphoreType.DMA((chunks,)),
            pltpu.SemaphoreType.DMA((3,)),
            pltpu.SemaphoreType.DMA((2,)),
            pltpu.SemaphoreType.DMA((2,)),
            pltpu.SemaphoreType.REGULAR((len(STEPS), 2)),
            pltpu.SemaphoreType.DMA((window * CORES,)),
            pltpu.SemaphoreType.DMA((window * CORES,)),
            pltpu.SemaphoreType.DMA((chips,)),
            pltpu.SemaphoreType.DMA((chips,)),
            pltpu.SemaphoreType.DMA((chips,)),
        ],
        compiler_params=pltpu.CompilerParams(collective_id=0, has_side_effects=True),
    )(queries, lengths, k_cache.reshape(rows, width), v_cache.reshape(rows, width))
    return result.reshape(requests, group, width)


def solution(mesh):
    return jax.shard_map(
        shards,
        mesh=mesh,
        in_specs=(
            P(("group", "sub"), "head", None),
            P(("group", "sub")),
            P(("group", "seq", "sub"), "head", None),
            P(("group", "seq", "sub"), "head", None),
        ),
        out_specs=P("group", ("head", "sub"), None),
        check_vma=False,
    )
```

time: 68.8 us -> 74 us (1.076)
  Pallas kernels: 67.2 us -> 72.3 us
    pallas_call x1, Pallas kernels: 67.2 us -> 72.3 us  [shards(): pl.pallas_call(functools.partial(kernel, chips), out_shape=jax.ShapeDtype...]
where the time goes in v2:
time: 74 us; the launch traced here: 73.7 us
  Pallas kernels  72.3 us (98%)
  local copies, waits for them, and re-layouts  1.33 us (2%)
    pallas_call x1, Pallas kernels, shards(): pl.pallas_call(functools.partial(kernel, chips), out_shape=jax.ShapeDtype...  72.3 us

profile of v2, /device:TPU:38, one launch (start us, length us, event | category | flops | bytes accessed | tf_op | source)
XLA Modules:
  0.0 73.7 jit_solution(6606564009396301668)
XLA Ops:
  0.0 72.3 %shard_map.46 = bf16[64,128]{1,0:T(8,128)(2,1)} custom-call(bf16[8,8,128]{2,1,0:T(8,128)(2,1)} %q_hbm.1, s32[8]{0:T(128)} %len_hbm.1, bf16[8192,128]{1,0:T(8,128)(2,1)} %bitcast.3, bf16[8192,128]{1,0:T(8,128)(2,1)} %bitcast.4), custom_call_target="tpu_custom_call" | custom-call | tf_op jit(solution)/shard_map/pallas_call | solution.py:339
  72.3 1.3 %copy.6 = bf16[16,4,128]{2,1,0:T(4,128)(2,1)} copy(bf16[16,4,128]{2,1,0:T(4,128)(2,1)} %bitcast.5) | data formatting | bytes 32768

commit v3 on v2

--- a/solution.py
+++ b/solution.py
@@ -12,7 +12,7 @@
 CORES = 2
 NEG = -1e30
 MESH = pl.DeviceIdType.MESH
-STEPS = (1, 2, 4, 4)
+STEPS = (1, 2, 4)
 PARTS = 4
 
 
@@ -144,14 +144,15 @@
         firsts.append(begins)
 
     q_away.wait()
+    for i in range(chunks):
+        k_copy(i).wait()
+        v_copy(i).wait()
     lane_head = lax.rem(lax.broadcasted_iota(jnp.int32, (heads, page_rows), 1), CORES)
     row_head = lax.broadcasted_iota(jnp.int32, (heads, page_rows), 0) // group
     mine = lane_head == row_head
     scale = float(width) ** -0.5
     running = None
     for p in range(pages):
-        if p % chunk_pages == 0:
-            k_copy(p // chunk_pages).wait()
         keys = kbuf[p * page_rows : (p + 1) * page_rows, :]
         values = lax.dot_general(
             qbuf[owners[p]], keys, (((1,), (1,)), ((), ())), preferred_element_type=jnp.float32
@@ -170,8 +171,6 @@
 
     summed = gathered = None
     for p in range(pages):
-        if p % chunk_pages == 0:
-            v_copy(p // chunk_pages).wait()
         last = jnp.clip(start_sm[owners[p] + 1] - base - 1, 0, pages - 1)
         lift = jnp.exp(page_max[p] - rounded(run_max[last]))
         values = vbuf[p * page_rows : (p + 1) * page_rows, :]
@@ -237,8 +236,6 @@
             part_copies.append(part_copy(o, k, len(part_copies)))
             part_copies[-1].start()
     got[reach * CORES + s] = sent[lax.rem(c, PARTS), s]
-    wait_level(2)
-    signal_level(3)
     for o in offsets:
         for k in range(CORES) if o else (1 - s,):
             part_arrival(o, k).wait_recv()
@@ -268,23 +265,33 @@
     def arrived(origin):
         spread_copy(g_send.at[0], origin, chip(1)).wait_recv()
 
-    wait_level(3)
+    wait_level(2)
     beyond = chips // 2 - far
-    direct = [o for n in range(1, far + 1) for o in (n, -n)]
+    direct = [o for n in range(far, 0, -1) for o in (n, -n)]
+    for o in (far, -far):
+        spread_copy(g_send.at[chip(o)], c, chip(o)).start()
     for to in range(chips):
         ahead = lax.rem(to - c + chips, chips)
 
-        @pl.when((ahead > 0) & ((ahead <= far) | (ahead >= chips - far)))
+        @pl.when(((ahead > 0) & (ahead < far)) | (ahead > chips - far))
         def _():
             spread_copy(g_send.at[to], c, to).start()
 
     def upward(act):
-        for n in range(1, beyond + 1):
-            act(spread_copy(h_send.at[n - 1], chip(-far), chip(n)))
+        for to in range(chips):
+            ahead = lax.rem(to - c + chips, chips)
+
+            @pl.when((ahead > 0) & (ahead <= beyond))
+            def _():
+                act(spread_copy(h_send.at[to], chip(-far), to))
 
     def downward(act):
-        for n in range(1, beyond):
-            act(spread_copy(h_send.at[beyond + n - 1], chip(far), chip(-n)))
+        for to in range(chips):
+            ahead = lax.rem(to - c + chips, chips)
+
+            @pl.when(ahead > chips - beyond)
+            def _():
+                act(spread_copy(h_send.at[to], chip(far), to))
 
     @pl.when(c < chips // 2)
     def _():

time: 74 us -> 65.8 us (0.89)
  Pallas kernels: 72.3 us -> 64.2 us
    pallas_call x1, Pallas kernels: 72.3 us -> 64.2 us  [shards(): pl.pallas_call(functools.partial(kernel, chips), out_shape=jax.ShapeDtype...]
where the time goes in v3:
time: 65.8 us; the launch traced here: 65.6 us
  Pallas kernels  64.2 us (98%)
  local copies, waits for them, and re-layouts  1.33 us (2%)
    pallas_call x1, Pallas kernels, shards(): pl.pallas_call(functools.partial(kernel, chips), out_shape=jax.ShapeDtype...  64.2 us
    unnamed x1, local copies, waits for them, and re-layouts  1.33 us

profile of v3, /device:TPU:38, one launch (start us, length us, event | category | flops | bytes accessed | tf_op | source)
XLA Modules:
  0.0 65.6 jit_solution(13093967789847237387)
XLA Ops:
  0.0 64.2 %shard_map.46 = bf16[64,128]{1,0:T(8,128)(2,1)} custom-call(bf16[8,8,128]{2,1,0:T(8,128)(2,1)} %q_hbm.1, s32[8]{0:T(128)} %len_hbm.1, bf16[8192,128]{1,0:T(8,128)(2,1)} %bitcast.3, bf16[8192,128]{1,0:T(8,128)(2,1)} %bitcast.4), custom_call_target="tpu_custom_call" | custom-call | tf_op jit(solution)/shard_map/pallas_call | solution.py:346
  64.2 1.3 %copy.6 = bf16[16,4,128]{2,1,0:T(4,128)(2,1)} copy(bf16[16,4,128]{2,1,0:T(4,128)(2,1)} %bitcast.5) | data formatting | bytes 32768

commit v4 on v3

--- a/solution.py
+++ b/solution.py
@@ -64,7 +64,8 @@
     chunks = k_sem.shape[0]
     chunk_rows = rows // chunks
     chunk_pages = pages // chunks
-    per_part = requests // PARTS
+    slots = requests // 2
+    per_part = slots // PARTS
     reach = got.shape[0] // (2 * CORES)
     far = sum(STEPS) + 1
 
@@ -169,6 +170,20 @@
     wait_level(0)
     signal_level(1)
 
+    offsets = [o for n in range(reach, 0, -1) for o in (n, -n)] + [0]
+    chosen = []
+    for o in offsets:
+        picks = []
+        for i in range(per_part):
+            slot = lax.rem(chip(o), PARTS) * per_part + i
+            home = start_sm[slot + slots] // (pages * CORES)
+            later = lax.rem(chip(o) - home + chips, chips) < PARTS
+            r = jnp.where(later, slot + slots, slot)
+            begin = jnp.maximum(start_sm[r] - base, 0)
+            end = jnp.minimum(start_sm[r + 1] - base, pages)
+            picks.append((end > begin, jnp.clip(end - 1, 0, pages - 1)))
+        chosen.append(picks)
+
     summed = gathered = None
     for p in range(pages):
         last = jnp.clip(start_sm[owners[p] + 1] - base - 1, 0, pages - 1)
@@ -182,40 +197,26 @@
         run_sum[p] = summed
 
     lane = lax.broadcasted_iota(jnp.int32, (heads, width), 1)
-    half = lax.rem(lane, width // 2)
-    tops, sums, outs = [], [], []
-    for r in range(requests):
-        begin = jnp.maximum(starts[r] - base, 0)
-        end = jnp.minimum(start_sm[r + 1] - base, pages)
-        here = end > begin
-        last = jnp.clip(end - 1, 0, pages - 1)
-        peak = rounded(jnp.where(here, run_max[last], NEG))
-        weights = jnp.where(here, run_sum[last], 0.0)
-        high = weights.astype(jnp.bfloat16).astype(jnp.float32)
-        tops.append(jnp.where(half < 16, peak, jnp.where(half < 32, high, weights - high)))
-        outs.append(jnp.where(here, run_out[last], 0.0))
-
-    for j in range(PARTS):
-        members = range(j * per_part, (j + 1) * per_part)
+    for n, picks in enumerate(chosen):
+        tops, outs = [], []
+        for here, last in picks:
+            peak = rounded(jnp.where(here, run_max[last], NEG))
+            weights = jnp.where(here, run_sum[last], 0.0)
+            high = rounded(weights)
+            tops.append(jnp.where(lane < 16, peak, jnp.where(lane < 32, high, weights - high)))
+            outs.append(jnp.where(here, run_out[last], 0.0))
         for k in range(CORES):
             cut = slice(k * group, (k + 1) * group)
-            numbers = jnp.concatenate([outs[r][cut] for r in members], axis=0)
-            lower, upper = (
-                jnp.concatenate([tops[r][cut] for r in some], axis=0)
-                for some in (members[: per_part // 2], members[per_part // 2 :])
-            )
-            stats = jnp.where(lane < width // 2, lower, upper)
-            sent[j, k] = jnp.concatenate([numbers, stats], axis=0).astype(jnp.bfloat16)
+            sent[n, k] = jnp.concatenate([t[cut] for t in outs + tops], axis=0).astype(jnp.bfloat16)
 
     wait_level(1)
     signal_level(2)
 
     part_rows = per_part * group
-    offsets = [o for n in range(reach, 0, -1) for o in (n, -n)] + [0]
 
     def part_copy(o, k, n):
         return pltpu.make_async_remote_copy(
-            src_ref=sent.at[lax.rem(chip(o), PARTS), k],
+            src_ref=sent.at[offsets.index(o), k],
             dst_ref=got.at[(reach - o) * CORES + s],
             send_sem=r_send.at[n],
             recv_sem=r_recv.at[(reach - o) * CORES + s],
@@ -235,26 +236,21 @@
         for k in range(CORES) if o else (1 - s,):
             part_copies.append(part_copy(o, k, len(part_copies)))
             part_copies[-1].start()
-    got[reach * CORES + s] = sent[lax.rem(c, PARTS), s]
+    got[reach * CORES + s] = sent[len(offsets) - 1, s]
     for o in offsets:
         for k in range(CORES) if o else (1 - s,):
             part_arrival(o, k).wait_recv()
 
-    slots = got.shape[0]
-    stats = [got[i, part_rows:, :].astype(jnp.float32) for i in range(slots)]
+    parts = [got[i].astype(jnp.float32) for i in range(got.shape[0])]
+    stats = [part[part_rows:] for part in parts]
     peak = functools.reduce(jnp.maximum, stats)
-    blocks = []
-    for t in range(2):
-        first = t * width // 2
-        numer, denom = 0.0, 0.0
-        for i in range(slots):
-            lift = jnp.exp(stats[i][:, first : first + 1] - peak[:, first : first + 1])
-            part = got[i, t * part_rows // 2 : (t + 1) * part_rows // 2, :]
-            numer = numer + lift * part.astype(jnp.float32)
-            denom = denom + lift * stats[i]
-        denom = denom[:, first + 16 : first + 17] + denom[:, first + 32 : first + 33]
-        blocks.append(numer / jnp.where(denom > 0.0, denom, 1.0))
-    final[c] = jnp.concatenate(blocks, axis=0).astype(jnp.bfloat16)
+    numer, denom = 0.0, 0.0
+    for part, stat in zip(parts, stats):
+        lift = jnp.exp(stat[:, 0:1] - peak[:, 0:1])
+        numer = numer + lift * part[:part_rows]
+        denom = denom + lift * stat
+    denom = denom[:, 16:17] + denom[:, 32:33]
+    final[c] = (numer / jnp.where(denom > 0.0, denom, 1.0)).astype(jnp.bfloat16)
 
     def spread_copy(sem, origin, to):
         return pltpu.make_async_remote_copy(
@@ -312,14 +308,14 @@
             arrived(chip(n))
 
     row_request = lax.broadcasted_iota(jnp.int32, (part_rows, width), 0) // group
-    for j in range(PARTS):
+    for t in range(requests // per_part):
         block = None
         for i in range(per_part):
-            home = starts[j * per_part + i] // (pages * CORES)
-            home = home + lax.rem(j - lax.rem(home, PARTS) + PARTS, PARTS)
+            home = starts[t * per_part + i] // (pages * CORES)
+            home = home + lax.rem(t % PARTS - lax.rem(home, PARTS) + PARTS, PARTS)
             piece = final[lax.rem(home, chips)].astype(jnp.float32)
             block = piece if i == 0 else jnp.where(row_request == i, piece, block)
-        out_ref[j * part_rows : (j + 1) * part_rows, :] = block.astype(jnp.bfloat16)
+        out_ref[t * part_rows : (t + 1) * part_rows, :] = block.astype(jnp.bfloat16)
 
     for n in range(len(part_copies)):
         part_copies[n].wait_send()
@@ -340,7 +336,9 @@
     page_rows = PAGE * key_heads
     span = -(-(LONGEST - 1) // (pages * CORES))
     window = 2 * span + 1
-    part_rows = requests // PARTS * group
+    part_rows = requests // 2 // PARTS * group
+    elsewhere = -(-(chips * pages * CORES - PARTS * pages * CORES - LONGEST + 1) // LONGEST)
+    assert requests - elsewhere <= requests // 2
     chunks = 4
     bf16, f32 = jnp.bfloat16, jnp.float32
     result = pl.pallas_call(
@@ -358,8 +356,8 @@
             pltpu.VMEM((pages, heads, width), f32),
             pltpu.VMEM((pages, heads, width), f32),
             pltpu.VMEM((pages, heads, width), f32),
-            pltpu.VMEM((PARTS, CORES, part_rows * 3 // 2, width), bf16),
-            pltpu.VMEM((window * CORES, part_rows * 3 // 2, width), bf16),
+            pltpu.VMEM((window, CORES, 2 * part_rows, width), bf16),
+            pltpu.VMEM((window * CORES, 2 * part_rows, width), bf16),
             pltpu.VMEM((chips, part_rows, width), bf16),
             pltpu.VMEM((own_requests,), jnp.int32),
             pltpu.SMEM((CORES, own_requests), jnp.int32),

time: 65.8 us -> 64.8 us (0.985)
  Pallas kernels: 64.2 us -> 63.2 us
    pallas_call x1, Pallas kernels: 64.2 us -> 63.2 us  [shards(): pl.pallas_call(functools.partial(kernel, chips), out_shape=jax.ShapeDtype...]
where the time goes in v4:
time: 64.8 us; the launch traced here: 64.5 us
  Pallas kernels  63.2 us (98%)
  local copies, waits for them, and re-layouts  1.33 us (2%)
    pallas_call x1, Pallas kernels, shards(): pl.pallas_call(functools.partial(kernel, chips), out_shape=jax.ShapeDtype...  63.2 us
    unnamed x1, local copies, waits for them, and re-layouts  1.33 us

profile of v4, /device:TPU:38, one launch (start us, length us, event | category | flops | bytes accessed | tf_op | source)
XLA Modules:
  0.0 64.5 jit_solution(7191655401209762658)
XLA Ops:
  0.0 63.2 %shard_map.46 = bf16[64,128]{1,0:T(8,128)(2,1)} custom-call(bf16[8,8,128]{2,1,0:T(8,128)(2,1)} %q_hbm.1, s32[8]{0:T(128)} %len_hbm.1, bf16[8192,128]{1,0:T(8,128)(2,1)} %bitcast.3, bf16[8192,128]{1,0:T(8,128)(2,1)} %bitcast.4), custom_call_target="tpu_custom_call" | custom-call | tf_op jit(solution)/shard_map/pallas_call | solution.py:344
  63.2 1.3 %copy.6 = bf16[16,4,128]{2,1,0:T(4,128)(2,1)} copy(bf16[16,4,128]{2,1,0:T(4,128)(2,1)} %bitcast.5) | data formatting | bytes 32768

commit v5 on v4

--- a/solution.py
+++ b/solution.py
@@ -39,6 +39,7 @@
     sent,
     got,
     final,
+    mixed,
     len_vm,
     len_sm,
     start_sm,
@@ -262,7 +263,6 @@
         spread_copy(g_send.at[0], origin, chip(1)).wait_recv()
 
     wait_level(2)
-    beyond = chips // 2 - far
     direct = [o for n in range(far, 0, -1) for o in (n, -n)]
     for o in (far, -far):
         spread_copy(g_send.at[chip(o)], c, chip(o)).start()
@@ -273,47 +273,75 @@
         def _():
             spread_copy(g_send.at[to], c, to).start()
 
-    def upward(act):
+    half = far // 2
+    row_request = lax.broadcasted_iota(jnp.int32, (part_rows, width), 0) // group
+
+    def mixed_copy(side, to):
+        place = (1 + side) * chips + c
+        return pltpu.make_async_remote_copy(
+            src_ref=mixed.at[side], dst_ref=final.at[place], send_sem=h_send.at[to],
+            recv_sem=g_recv.at[place], device_id={"seq": to, "sub": s}, device_id_type=MESH,
+        )
+
+    def relay(side):
+        way = 1 - 2 * side
+        nearer, away = chip(-way * half), chip(-way * far)
+        arrived(nearer)
+        arrived(away)
+        pick = None
+        for i in range(per_part):
+            slot = lax.rem(c, PARTS) * per_part + i
+            count = jnp.int32(0)
+            for r in (slot, slot + slots):
+                home = start_sm[r] // (pages * CORES)
+                count = count + (lax.rem(nearer - home + chips, chips) < PARTS).astype(jnp.int32)
+            pick = count if i == 0 else jnp.where(row_request == i, count, pick)
+        block = jnp.where(
+            jnp.broadcast_to(pick, (part_rows, width)) > 0,
+            final[nearer].astype(jnp.float32),
+            final[away].astype(jnp.float32),
+        )
+        mixed[side] = block.astype(jnp.bfloat16)
         for to in range(chips):
-            ahead = lax.rem(to - c + chips, chips)
-
-            @pl.when((ahead > 0) & (ahead <= beyond))
+            ahead = lax.rem(way * (to - c) + chips, chips)
+
+            @pl.when((ahead > half) & (ahead <= far))
             def _():
-                act(spread_copy(h_send.at[to], chip(-far), to))
-
-    def downward(act):
-        for to in range(chips):
-            ahead = lax.rem(to - c + chips, chips)
-
-            @pl.when(ahead > chips - beyond)
-            def _():
-                act(spread_copy(h_send.at[to], chip(far), to))
+                mixed_copy(side, to).start()
 
     @pl.when(c < chips // 2)
     def _():
-        arrived(chip(far))
-        downward(lambda copy: copy.start())
-        arrived(chip(-far))
-        upward(lambda copy: copy.start())
+        relay(1)
+        relay(0)
 
     @pl.when(c >= chips // 2)
     def _():
-        arrived(chip(-far))
-        upward(lambda copy: copy.start())
-        arrived(chip(far))
-        downward(lambda copy: copy.start())
-
-    for n in range(1, chips):
-        if n not in (far, chips - far):
+        relay(0)
+        relay(1)
+
+    for n in range(1, far + 1):
+        if n not in (half, far):
             arrived(chip(n))
-
-    row_request = lax.broadcasted_iota(jnp.int32, (part_rows, width), 0) // group
+            arrived(chip(-n))
+    for n in range(half + 1, far + 1):
+        arrived(chips + chip(-n))
+        arrived(2 * chips + chip(n))
+
     for t in range(requests // per_part):
         block = None
         for i in range(per_part):
             home = starts[t * per_part + i] // (pages * CORES)
             home = home + lax.rem(t % PARTS - lax.rem(home, PARTS) + PARTS, PARTS)
-            piece = final[lax.rem(home, chips)].astype(jnp.float32)
+            home = lax.rem(home, chips)
+            ahead = lax.rem(c - home + chips, chips)
+            behind = chips - ahead
+            above = home + jnp.where(ahead <= far + half, half, far)
+            below = home + chips - jnp.where(behind <= far + half, half, far)
+            place = jnp.where(
+                ahead <= 2 * far, chips + lax.rem(above, chips), 2 * chips + lax.rem(below, chips)
+            )
+            place = jnp.where((ahead <= far) | (behind <= far), home, place)
+            piece = final[place].astype(jnp.float32)
             block = piece if i == 0 else jnp.where(row_request == i, piece, block)
         out_ref[t * part_rows : (t + 1) * part_rows, :] = block.astype(jnp.bfloat16)
 
@@ -321,8 +349,9 @@
         part_copies[n].wait_send()
     for o in direct:
         spread_copy(g_send.at[chip(o)], c, chip(o)).wait_send()
-    upward(lambda copy: copy.wait_send())
-    downward(lambda copy: copy.wait_send())
+    for n in range(half + 1, far + 1):
+        mixed_copy(0, chip(n)).wait_send()
+        mixed_copy(1, chip(-n)).wait_send()
 
 
 def shards(queries, lengths, k_cache, v_cache):
@@ -358,7 +387,8 @@
             pltpu.VMEM((pages, heads, width), f32),
             pltpu.VMEM((window, CORES, 2 * part_rows, width), bf16),
             pltpu.VMEM((window * CORES, 2 * part_rows, width), bf16),
-            pltpu.VMEM((chips, part_rows, width), bf16),
+            pltpu.VMEM((3 * chips, part_rows, width), bf16),
+            pltpu.VMEM((2, part_rows, width), bf16),
             pltpu.VMEM((own_requests,), jnp.int32),
             pltpu.SMEM((CORES, own_requests), jnp.int32),
             pltpu.SMEM((requests + 1,), jnp.int32),
@@ -372,7 +402,7 @@
             pltpu.SemaphoreType.DMA((window * CORES,)),
             pltpu.SemaphoreType.DMA((chips,)),
             pltpu.SemaphoreType.DMA((chips,)),
-            pltpu.SemaphoreType.DMA((chips,)),
+            pltpu.SemaphoreType.DMA((3 * chips,)),
         ],
         compiler_params=pltpu.CompilerParams(collective_id=0, has_side_effects=True),
     )(queries, lengths, k_cache.reshape(rows, width), v_cache.reshape(rows, width))

time: 64.8 us -> 66.3 us (1.023)
  Pallas kernels: 63.2 us -> 64.6 us
    pallas_call x1, Pallas kernels: 63.2 us -> 64.6 us  [shards(): pl.pallas_call(functools.partial(kernel, chips), out_shape=jax.ShapeDtype...]
where the time goes in v5:
time: 66.3 us; the launch traced here: 65.9 us
  Pallas kernels  64.6 us (97%)
  local copies, waits for them, and re-layouts  1.33 us (2%)
    pallas_call x1, Pallas kernels, shards(): pl.pallas_call(functools.partial(kernel, chips), out_shape=jax.ShapeDtype...  64.6 us
    unnamed x1, local copies, waits for them, and re-layouts  1.33 us

profile of v5, /device:TPU:38, one launch (start us, length us, event | category | flops | bytes accessed | tf_op | source)
XLA Modules:
  0.0 65.9 jit_solution(2767424225432363892)
XLA Ops:
  0.0 64.6 %shard_map.46 = bf16[64,128]{1,0:T(8,128)(2,1)} custom-call(bf16[8,8,128]{2,1,0:T(8,128)(2,1)} %q_hbm.1, s32[8]{0:T(128)} %len_hbm.1, bf16[8192,128]{1,0:T(8,128)(2,1)} %bitcast.3, bf16[8192,128]{1,0:T(8,128)(2,1)} %bitcast.4), custom_call_target="tpu_custom_call" | custom-call | tf_op jit(solution)/shard_map/pallas_call | solution.py:373
  64.6 1.3 %copy.6 = bf16[16,4,128]{2,1,0:T(4,128)(2,1)} copy(bf16[16,4,128]{2,1,0:T(4,128)(2,1)} %bitcast.5) | data formatting | bytes 32768
